TPU v7x, 1024 devices: a whole 4x8x16 slice. The times are simulated.
1024 devices in a mesh: dp: 64 (over x, y, core), tensor: 16 (over z).
Axes of the slice: x: 4, y: 8, z: 16, core: 2. Of those that a mesh axis runs over, the one named last changes fastest.
Arguments:
- tokens: bfloat16 [8192, 6144], P('dp', 'tensor'), may hold values from -6 to 6
- expert_ids: int32 [8192, 2], P('dp'), may hold values from 0 to 63, all different within a row; in each aligned block of 128 rows (0 to 127, 128 to 255, ...) at most 5 rows name the same one
- combine: float32 [8192, 2], P('dp'), may hold values from 0.2 to 1
- up_weight: bfloat16 [64, 6144, 2048], P('dp', None, 'tensor'), may hold values from -0.078125 to 0.078125
- down_weight: bfloat16 [64, 2048, 6144], P('dp', 'tensor'), may hold values from -0.1875 to 0.1875
Outputs:
- mixed: bfloat16 [8192, 6144], P('dp', 'tensor')
Inputs may be any that keep to these rules, and one draw needn't show every extreme that they name: `expert_ids`: each token names 2 different experts. Among the 128 tokens of one index of dp, no expert is named more than 5 times, a bound that some block reaches.
All inputs are finite; a program needn't handle non-finite values.
Results may differ from a plain program's by a relative error of at most 0.019.
Values may be sent and summed in bfloat16 or wider, within the bound.
No kernel may reach another device: no remote copies, remote signals or barrier semaphores. Data moves between devices by JAX's collectives and lax.ppermute only.
A program may use at most 32 MiB of HBM per device.

v0:
```python
import jax
import jax.numpy as jnp
from jax import lax
from jax.sharding import PartitionSpec as P


def on_device(tokens, expert_ids, combine, up_weight, down_weight):
    tok_rows, feat = tokens.shape
    experts = lax.axis_size("dp")
    capacity = 5 * tok_rows // (2 * experts)
    picks = expert_ids.shape[1]
    flat_ids = expert_ids.reshape(-1)
    onehot = (flat_ids[:, None] == jnp.arange(experts, dtype=jnp.int32)[None, :]).astype(jnp.int32)
    earlier = jnp.cumsum(onehot, axis=0) - onehot
    slots = jnp.sum(earlier * onehot, axis=1)
    position = flat_ids * capacity + slots
    placer = (position[:, None] == jnp.arange(experts * capacity, dtype=jnp.int32)[None, :]).astype(
        jnp.bfloat16
    )
    repeated = jnp.repeat(tokens, picks, axis=0)
    outgoing = jnp.einsum("ps,pf->sf", placer, repeated, preferred_element_type=jnp.float32)
    outgoing = outgoing.astype(jnp.bfloat16).reshape(experts, capacity, feat)
    up_local = up_weight[0]
    down_local = down_weight[0]
    received = lax.all_to_all(outgoing, "dp", split_axis=0, concat_axis=0, tiled=True)
    sources, count, width = received.shape
    row_count = sources * count
    flat_rows = received.reshape(row_count, width)
    accum = jnp.dot(
        lax.all_gather(flat_rows, "tensor", axis=1, tiled=True),
        up_local,
        preferred_element_type=jnp.float32,
    )
    hidden = jax.nn.silu(accum).astype(jnp.bfloat16)
    partial_value = jnp.dot(hidden, down_local, preferred_element_type=jnp.float32)
    result = lax.psum_scatter(
        partial_value.astype(jnp.bfloat16), "tensor", scatter_dimension=1, tiled=True
    )
    returned = lax.all_to_all(
        result.reshape(sources, count, width), "dp", split_axis=0, concat_axis=0, tiled=True
    )
    picked = jnp.dot(
        placer, returned.reshape(experts * capacity, feat), preferred_element_type=jnp.float32
    )
    picked = picked.reshape(tok_rows, picks, feat)
    mixed = jnp.sum(picked * combine[:, :, None], axis=1)
    return mixed.astype(jnp.bfloat16)


def solution(mesh):
    placed = (
        P("dp", "tensor"),
        P("dp", None),
        P("dp", None),
        P("dp", None, "tensor"),
        P("dp", "tensor", None),
    )
    return jax.shard_map(
        on_device, mesh=mesh, in_specs=placed, out_specs=P("dp", "tensor"), check_vma=False
    )
```

profile of v0, /device:TPU:1, one launch (start us, length us, event | category | flops | bytes accessed | tf_op | source)
XLA Modules:
  0.0 254.3 jit_solution(4979695873370841338)
XLA Ops:
  6.5 0.0 copy-start
  6.5 0.0 all-gather.2.cloned.1.call-start
  6.5 0.9 copy.18
  7.4 0.1 eq.60
  7.6 0.1 eq.64
  7.7 0.6 reduce-window.6
  8.4 0.2 slice_reduce_fusion
  8.6 0.1 fusion.15
  8.7 1.0 broadcast_in_dim.2
  9.7 0.1 reshape.68
  9.8 0.4 convolution_convert_fusion.1
  10.2 0.1 reshape.69
  10.3 32.0 %all_to_all.10 = bf16[64,5,384]{2,1,0:T(8,128)(2,1)S(1)} all-to-all(bf16[64,5,384]{2,1,0:T(8,128)(2,1)S(1)} %reshape.69), channel_id=1, replica_groups=mesh['dp'=64,'tensor'=16] {'dp'}, dimensions={0} | all-to-all | bytes 491520 | tf_op jit(solution)/shard_map/all_to_all | solution.py:25
  42.3 0.8 reshape.70
  43.1 0.0 all-gather.2.cloned.1.call-update
  43.1 0.0 reduce-scatter.4.cloned.1.call-start
  43.2 70.7 %all-gather.2.cloned.1.call-done = bf16[320,6144]{1,0:T(8,128)(2,1)} async-done(((bf16[320,384]{1,0:T(8,128)(2,1)}), bf16[320,6144]{1,0:T(8,128)(2,1)}) %all-gather.2.cloned.1.call-update) | async-done | bytes 3932176 | tf_op jit(solution)/shard_map/all_gather | solution.py:30
  113.9 0.0 copy-done
  113.9 8.7 %convolution_convert_fusion = bf16[320,6144]{1,0:T(8,128)(2,1)} fusion(bf16[1,128,6144]{2,1,0:T(8,128)(2,1)S(1)} %copy-done, bf16[320,6144]{1,0:T(8,128)(2,1)} %all-gather.2.cloned.1.call-done, bf16[1,6144,128]{2,1,0:T(8,128)(2,1)} %param.8), kind=kOutput, calls=%fused_computation | convolution fusion | flops 1008803840 | bytes 11010048 | tf_op jit(solution)/shard_map/dot_general | solution.py:35
  122.6 6.4 %copy.22 = bf16[320,6144]{0,1:T(8,128)(2,1)} copy(bf16[320,6144]{1,0:T(8,128)(2,1)} %convolution_convert_fusion) | data formatting | bytes 7864320
  129.0 0.0 reduce-scatter.4.cloned.1.call-update
  129.0 80.4 %reduce-scatter.4.cloned.1.call-done = bf16[384,320]{1,0:T(8,128)(2,1)} async-done(((bf16[6144,320]{1,0:T(8,128)(2,1)}), bf16[384,320]{1,0:T(8,128)(2,1)}) %reduce-scatter.4.cloned.1.call-update) | async-done | bytes 245776
  209.4 1.1 copy.23
  210.5 0.8 reshape.71
  211.4 20.4 %all-to-all-start.1 = ((bf16[64,5,384]{2,1,0:T(8,128)(2,1)}), bf16[64,5,384]{2,1,0:T(8,128)(2,1)S(1)}, u32[]{:S(2)}, u32[]{:S(2)}) async-start(bf16[64,5,384]{2,1,0:T(8,128)(2,1)} %reshape.71), calls=%async_computation.1 | async-start | bytes 786432 | tf_op jit(solution)/shard_map/all_to_all | solution.py:39
  231.8 0.1 reduce_sum.21
  231.9 0.1 copy.21
  232.0 0.0 copy-done.1
  232.0 14.3 %all-to-all-done.1 = bf16[64,5,384]{2,1,0:T(8,128)(2,1)S(1)} async-done(((bf16[64,5,384]{2,1,0:T(8,128)(2,1)}), bf16[64,5,384]{2,1,0:T(8,128)(2,1)S(1)}, u32[]{:S(2)}, u32[]{:S(2)}) %all-to-all-start.1) | async-done | bytes 245792 | tf_op jit(solution)/shard_map/all_to_all | solution.py:39
  246.3 0.1 reshape.73
  246.4 0.0 copy-done.2
  246.4 1.0 fusion.3
  (7 shorter events, 0.1 us)
Async XLA Ops:
  6.5 107.3 %copy-start = (bf16[1,128,6144]{2,1,0:T(8,128)(2,1)S(1)}, bf16[1,128,6144]{2,1,0:T(8,128)(2,1)}, u32[]{:S(2)}) copy-start(bf16[1,128,6144]{2,1,0:T(8,128)(2,1)} %param.9) | copy-start | bytes 4718596
  6.5 107.3 %all-gather.2.cloned.1.call-start = ((), (), s32[]{:S(2)}) async-start(), calls=%async_computation.3 | async-start | bytes 4177920 | tf_op jit(solution)/shard_map/all_gather | solution.py:30
  43.1 166.3 %reduce-scatter.4.cloned.1.call-start = ((), (), s32[]{:S(2)}) async-start(), calls=%async_computation.4 | async-start | bytes 5013504
  129.0 103.0 %copy-start.1 = (s32[128,2]{0,1:T(2,128)S(1)}, s32[128,2]{0,1:T(2,128)}, u32[]{:S(2)}) copy-start(s32[128,2]{0,1:T(2,128)} %param.6) | copy-start | bytes 3076
  129.0 117.4 %copy-start.2 = (f32[128,2]{0,1:T(2,128)S(1)}, f32[128,2]{0,1:T(2,128)}, u32[]{:S(2)}) copy-start(f32[128,2]{0,1:T(2,128)} %param.7) | copy-start | bytes 3076
  211.4 34.9 %all-to-all-start.1 = ((bf16[64,5,384]{2,1,0:T(8,128)(2,1)}), bf16[64,5,384]{2,1,0:T(8,128)(2,1)S(1)}, u32[]{:S(2)}, u32[]{:S(2)}) async-start(bf16[64,5,384]{2,1,0:T(8,128)(2,1)} %reshape.71), calls=%async_computation.1 | async-start | bytes 786432 | tf_op jit(solution)/shard_map/all_to_all | solution.py:39
Sparse Core Ops, SparseCore 0:
  43.2 70.5 all-gather.1
  129.2 80.1 reduce-scatter.3
where the time goes:
time: 255 us; the launch traced here: 254 us
  waiting for transfers between devices  165 us (65%)
  blocking collectives  32 us (13%)
  starting transfers between devices  20.4 us (8%)
  between operations  13.5 us (5%)
  local copies, waits for them, and re-layouts  12 us (5%)
  matrix products  10.1 us (4%)
    unnamed x3, waiting for transfers between devices  80.4 us
    all_gather x1, waiting for transfers between devices, on_device(): lax.all_gather(flat_rows, 'tensor', axis=1, tiled=True)  70.7 us
    all_to_all x1, blocking collectives, on_device(): lax.all_to_all(outgoing, 'dp', split_axis=0, concat_axis=0, tiled=True)  32 us
    all_to_all x1, starting transfers between devices, on_device(): lax.all_to_all(result.reshape(sources, count, width), 'dp', split_axis=0,...  20.4 us
    all_to_all x1, waiting for transfers between devices, on_device(): lax.all_to_all(result.reshape(sources, count, width), 'dp', split_axis=0,...  14.3 us
    dot_general x1, matrix products, on_device(): jnp.dot(hidden, down_local, preferred_element_type=jnp.float32)  8.75 us
    unnamed x9, local copies, waits for them, and re-layouts  8.44 us
  transfers between devices with their start and end apart: 3, of which 3 were waited for; matrix products, arithmetic and copies ran while one was open for 0% of the time, Pallas kernels for 0%

commit v1 on v0

v1 whole, which is shorter than its diff:
```python
import jax
import jax.numpy as jnp
from jax import lax
from jax.experimental.layout import Layout, with_layout_constraint
from jax.sharding import Mesh
from jax.sharding import PartitionSpec as P


LANES = 128
SCALE = 8192.0


def swap(value, axis, step):
    size = lax.axis_size(axis)
    return lax.ppermute(value, axis, [(i, i ^ step) for i in range(size)])


def shift(value, axis, step):
    size = lax.axis_size(axis)
    return lax.ppermute(value, axis, [(i, (i + step) % size) for i in range(size)])


def on_device(tokens, expert_ids, combine, up_weight, down_weight):
    tok_rows, feat = tokens.shape
    experts = lax.axis_size("dp")
    high, low = lax.axis_size("hi"), lax.axis_size("lo")
    capacity = 5 * tok_rows // (2 * experts)
    picks = expert_ids.shape[1]
    tiles = feat // LANES
    packed_rows = -(-(capacity * tiles) // 16) * 16
    row_count = experts * capacity

    down_local = down_weight[0]
    mine, group = lax.axis_index("lo"), lax.axis_index("hi")

    def share(step):
        cuts = []
        for turn in range(high):
            owner = (group + turn) % high * low + (mine ^ step)
            cuts.append(lax.dynamic_slice_in_dim(down_local, owner * feat, feat, axis=1))
        block = jnp.concatenate(cuts, axis=1)
        return with_layout_constraint(block, Layout(major_to_minor=(0, 1)))

    down_parts = [share(0)]
    for step in range(1, low):
        down_parts.append(swap(share(step), "lo", step))

    token = jnp.arange(tok_rows, dtype=jnp.int32)
    before = token[:, None] < token[None, :]
    slots = []
    for pick in range(picks):
        same = jnp.zeros((tok_rows, tok_rows), jnp.int32)
        for other in range(picks):
            same = same + (expert_ids[:, other][:, None] == expert_ids[:, pick][None, :])
        slots.append(jnp.sum(jnp.where(before, same, 0), axis=0))
    slots = jnp.stack(slots, axis=1)
    place = expert_ids * packed_rows + slots
    spots = jnp.arange(experts * packed_rows, dtype=jnp.int32)[None, :]

    def chosen(pick, tile):
        return place[:, pick][:, None] + tile * capacity == spots

    outgoing = jnp.zeros((experts * packed_rows, LANES), jnp.float32)
    for tile in range(tiles):
        both = (chosen(0, tile) | chosen(1, tile)).astype(jnp.bfloat16)
        outgoing = outgoing + jnp.einsum(
            "ts,tf->sf", both, tokens[:, tile * LANES : (tile + 1) * LANES],
            preferred_element_type=jnp.float32,
        )
    outgoing = outgoing.astype(jnp.bfloat16).reshape(experts, packed_rows, LANES)
    received = lax.all_to_all(outgoing, "dp", split_axis=0, concat_axis=0, tiled=True)
    received = received.reshape(experts * packed_rows, LANES)

    rows = jnp.arange(row_count, dtype=jnp.int32)
    row_spot = (rows // capacity) * packed_rows + rows % capacity

    def unpacker(tile):
        return (row_spot[:, None] + tile * capacity == spots).astype(jnp.bfloat16)

    flat_rows = jnp.concatenate(
        [
            jnp.dot(unpacker(tile), received, preferred_element_type=jnp.float32)
            for tile in range(tiles)
        ],
        axis=1,
    )
    scaled = (flat_rows * SCALE).astype(jnp.float16)
    gathered = lax.all_gather(scaled, ("hi", "lo"), axis=1, tiled=True)
    accum = jnp.dot(gathered.astype(jnp.bfloat16), up_weight[0], preferred_element_type=jnp.float32)
    hidden = jax.nn.silu(accum * (1.0 / SCALE)).astype(jnp.bfloat16)
    pieces = [hidden] + [swap(hidden, "lo", step) for step in range(1, low)]
    hidden = jnp.concatenate(pieces, axis=1)
    down_mine = jnp.concatenate(down_parts, axis=0)
    part = jnp.dot(hidden, down_mine, preferred_element_type=jnp.float32)

    keep, ahead, across, behind = [part[:, k * feat : (k + 1) * feat] for k in range(high)]
    half = row_count // 2
    across = across.astype(jnp.bfloat16)
    from_behind = shift(across[:half], "hi", 1)
    from_ahead = shift(across[half:], "hi", -1)
    ahead = jnp.concatenate([ahead[:half] + from_behind.astype(jnp.float32), ahead[half:]], axis=0)
    behind = jnp.concatenate([behind[:half], behind[half:] + from_ahead.astype(jnp.float32)], axis=0)
    one = shift(ahead.astype(jnp.bfloat16), "hi", 1)
    two = shift(behind.astype(jnp.bfloat16), "hi", -1)
    result = keep + one.astype(jnp.float32) + two.astype(jnp.float32)
    result = result.astype(jnp.bfloat16)

    packed = jnp.zeros((experts * packed_rows, LANES), jnp.float32)
    for tile in range(tiles):
        packed = packed + jnp.einsum(
            "rs,rf->sf", unpacker(tile), result[:, tile * LANES : (tile + 1) * LANES],
            preferred_element_type=jnp.float32,
        )
    packed = packed.astype(jnp.bfloat16).reshape(experts, packed_rows, LANES)
    returned = lax.all_to_all(packed, "dp", split_axis=0, concat_axis=0, tiled=True)
    returned = returned.reshape(experts * packed_rows, LANES)
    columns = []
    for tile in range(tiles):
        total = 0.0
        for pick in range(picks):
            one_hot = chosen(pick, tile).astype(jnp.bfloat16)
            row = jnp.dot(one_hot, returned, preferred_element_type=jnp.float32)
            total = total + row * combine[:, pick][:, None]
        columns.append(total)
    return jnp.concatenate(columns, axis=1).astype(jnp.bfloat16)


def solution(mesh):
    shape = mesh.devices.shape
    low = 4
    split = Mesh(mesh.devices.reshape(shape[0], shape[1] // low, low), ("dp", "hi", "lo"))
    tensor = ("hi", "lo")
    placed = (
        P("dp", tensor),
        P("dp", None),
        P("dp", None),
        P("dp", None, tensor),
        P("dp", tensor, None),
    )
    return jax.shard_map(
        on_device, mesh=split, in_specs=placed, out_specs=P("dp", tensor), check_vma=False
    )
```

time: 255 us -> 217 us (0.85)
  waiting for transfers between devices: 165 us -> 35.1 us
  starting transfers between devices: 20.4 us -> 81.6 us
  blocking collectives: 32 us -> 82 us
  between operations: 13.5 us -> 0.37 us
  local copies, waits for them, and re-layouts: 12 us -> 3.34 us
  matrix products: 10.1 us -> 13.2 us
    all_gather x0 -> x1, blocking collectives: none -> 82 us  [on_device(): gathered = lax.all_gather(scaled, ('hi', 'lo'), axis=1, tiled=True)]
    unnamed x3 -> x0, waiting for transfers between devices: 80.4 us -> none
    all_gather x1 -> x0, waiting for transfers between devices: 70.7 us -> none  [on_device(): lax.all_gather(flat_rows, 'tensor', axis=1, tiled=True)]
    ppermute x0 -> x10, starting transfers between devices: none -> 40.1 us  [the longest x6 21.7 us: swap(): return lax.ppermute(value, axis, [(i, i ^ step) for i in range(size)])]
    all_to_all x1 -> x0, blocking collectives: 32 us -> none  [on_device(): lax.all_to_all(outgoing, 'dp', split_axis=0, concat_axis=0, tiled=True)]
    all_to_all x1 -> x2, starting transfers between devices: 20.4 us -> 41.5 us  [the longest x1 26.3 us: on_device(): lax.all_to_all(packed, 'dp', split_axis=0, concat_axis=0, tiled=True)]
    ppermute x0 -> x10, waiting for transfers between devices: none -> 18.9 us  [the longest x4 16.8 us: shift(): lax.ppermute(value, axis, [(i, (i + step) % size) for i in range(size)])]
    unnamed x9 -> x14, local copies, waits for them, and re-layouts: 8.44 us -> 0.03 us
  transfers between devices with their start and end apart: 3 -> 12, of which waited for: 3 -> 7; matrix products, arithmetic and copies ran while one was open for 0% -> 2% of each run, Pallas kernels for 0% -> 0%
where the time goes in v1:
time: 217 us; the launch traced here: 216 us
  blocking collectives  82 us (38%)
  starting transfers between devices  81.6 us (38%)
  waiting for transfers between devices  35.1 us (16%)
  matrix products  13.2 us (6%)
  local copies, waits for them, and re-layouts  3.34 us (2%)
    all_gather x1, blocking collectives, on_device(): gathered = lax.all_gather(scaled, ('hi', 'lo'), axis=1, tiled=True)  82 us
    all_to_all x1, starting transfers between devices, on_device(): lax.all_to_all(packed, 'dp', split_axis=0, concat_axis=0, tiled=True)  26.3 us
    ppermute x6, starting transfers between devices, swap(): return lax.ppermute(value, axis, [(i, i ^ step) for i in range(size)])  21.7 us
    ppermute x4, starting transfers between devices, shift(): lax.ppermute(value, axis, [(i, (i + step) % size) for i in range(size)])  18.4 us
    ppermute x4, waiting for transfers between devices, shift(): lax.ppermute(value, axis, [(i, (i + step) % size) for i in range(size)])  16.8 us
    all_to_all x1, starting transfers between devices, on_device(): lax.all_to_all(outgoing, 'dp', split_axis=0, concat_axis=0, tiled=True)  15.2 us
    all_to_all x1, waiting for transfers between devices, on_device(): lax.all_to_all(packed, 'dp', split_axis=0, concat_axis=0, tiled=True)  11.9 us
  transfers between devices with their start and end apart: 12, of which 7 were waited for; matrix products, arithmetic and copies ran while one was open for 2% of the time, Pallas kernels for 0%

profile of v1, /device:TPU:1, one launch (start us, length us, event | category | flops | bytes accessed | tf_op | source)
XLA Modules:
  0.0 216.2 jit_solution(16601353901711613049)
XLA Ops:
  0.0 2.5 %dynamic-slice_bitcast_fusion.15 = (bf16[128,384]{1,0:T(8,128)(2,1)S(1)}, bf16[128,384]{1,0:T(8,128)(2,1)S(1)}, bf16[128,384]{1,0:T(8,128)(2,1)S(1)}, bf16[128,3...) fusion(bf16[1,128,6144]{2,1,0:T(8,128)(2,1)} %param.9, ...), kind=kLoop, calls=%fused_computation.111 | loop fusion | bytes 3145792 | tf_op jit(solution)/shard_map/dynamic_slice | solution.py:40
  2.5 4.8 %collective-permute-start.3 = (bf16[128,1536]{1,0:T(8,128)(2,1)S(1)}, bf16[128,1536]{1,0:T(8,128)(2,1)}, u32[]{:S(2)}, u32[]{:S(2)}) collective-permute-start(bf16[128,1536]{1,0:T(8,128)(2,1)S(1)} %pad_maximum_fusion), channel_id=1, source_target_pairs={{0,1},{1,0},{2,3},{3,2},{4,5},{5,4},{6,7},{7,6},{8,9},{9,8},{10,11... | collective-permute-start | bytes 1179656 | tf_op jit(solution)/shard_map/ppermute | solution.py:15
  7.5 0.4 fusion.47
  8.0 0.4 convolution_add_fusion.1
  8.4 1.1 fusion.25
  9.6 15.2 %all-to-all-start = ((bf16[64,16,128]{2,1,0:T(8,128)(2,1)}), bf16[64,16,128]{2,1,0:T(8,128)(2,1)S(1)}, u32[]{:S(2)}, u32[]{:S(2)}) async-start(bf16[64,16,128]{2,1,0:T(8,128)(2,1)} %bitcast.10), calls=%async_computation | async-start | bytes 524288 | tf_op jit(solution)/shard_map/all_to_all | solution.py:71
  24.8 1.9 collective-permute-start.4
  26.8 5.7 %collective-permute-start.5 = (bf16[128,1536]{1,0:T(8,128)(2,1)S(1)}, bf16[128,1536]{1,0:T(8,128)(2,1)}, u32[]{:S(2)}, u32[]{:S(2)}) collective-permute-start(bf16[128,1536]{1,0:T(8,128)(2,1)S(1)} %pad_maximum_fusion.2), channel_id=1, source_target_pairs={{0,3},{1,2},{2,1},{3,0},{4,7},{5,6},{6,5},{7,4},{8,11},{9,10},{10,... | collective-permute-start | bytes 1179656 | tf_op jit(solution)/shard_map/ppermute | solution.py:15
  32.6 4.2 %all-to-all-done = bf16[64,16,128]{2,1,0:T(8,128)(2,1)S(1)} async-done(((bf16[64,16,128]{2,1,0:T(8,128)(2,1)}), bf16[64,16,128]{2,1,0:T(8,128)(2,1)S(1)}, u32[]{:S(2)}, u32[]{:S(2)}) %all-to-all-start) | async-done | bytes 262176 | tf_op jit(solution)/shard_map/all_to_all | solution.py:71
  37.2 0.4 fusion.20
  37.6 0.4 fusion.22
  38.0 82.0 %all-gather.1 = f16[320,6144]{1,0:T(8,128)(2,1)S(1)} all-gather(f16[320,384]{1,0:T(8,128)(2,1)S(1)} %fusion.53), channel_id=1, replica_groups=mesh['dp'=64,'hi'=4,'lo'=4] {'hi','lo'}, dimensions={1}, use_global_device_ids=true | all-gather | bytes 4177920 | tf_op jit(solution)/shard_map/all_gather | solution.py:88
  120.1 1.2 multiply_convert_fusion
  121.3 1.9 collective-permute-start
  123.2 1.9 collective-permute-start.1
  125.2 5.4 %collective-permute-start.2 = (bf16[320,128]{1,0:T(8,128)(2,1)S(1)}, bf16[320,128]{1,0:T(8,128)(2,1)S(1)}, u32[]{:S(2)}, u32[]{:S(2)}) collective-permute-start(bf16[320,128]{1,0:T(8,128)(2,1)S(1)} %multiply_convert_fusion), channel_id=1, source_target_pairs={{0,3},{1,2},{2,1},{3,0},{4,7},{5,6},{6,5},{7,4},{8,11},{9,10},{10,... | collective-permute-start | bytes 245768 | tf_op jit(solution)/shard_map/ppermute | solution.py:15
  130.6 2.1 collective-permute-done.2
  132.8 4.2 %fusion.96 = (bf16[320,1536]{1,0:T(8,128)(2,1)S(1)}, f32[320,1536]{1,0:T(8,128)S(1)}) fusion(bf16[128,1536]{1,0:T(8,128)(2,1)} %collective-permute-done.5, bf16[128,1536]{1,0:T(8,128)(2,1)} %collective-permute-done.4, bf16[128,1536]{1,0:T(8,128)(2,1)} %collective-permute-done.3, bf16[128,384]{1,0:T(8,128)(2,1)S(1)} %copy-done.1, ...), kind=kOutput, calls=%fused_computation.149 | convolution fusion | flops 516128768 | bytes 4849664 | tf_op jit(solution)/shard_map/dot_general | solution.py:94
  137.0 3.2 %collective-permute-start.6 = (bf16[160,384]{1,0:T(8,128)(2,1)S(1)}, bf16[160,384]{1,0:T(8,128)(2,1)S(1)}, u32[]{:S(2)}, u32[]{:S(2)}) collective-permute-start(bf16[160,384]{1,0:T(8,128)(2,1)S(1)} %get-tuple-element.25), channel_id=1, source_target_pairs={{0,4},{4,8},{8,12},{12,0},{1,5},{5,9},{9,13},{13,1},{2,6},{6,10},{... | collective-permute-start | bytes 368648 | tf_op jit(solution)/shard_map/ppermute | solution.py:20
  140.2 6.0 %collective-permute-start.8 = (bf16[160,384]{1,0:T(8,128)(2,1)S(1)}, bf16[160,384]{1,0:T(8,128)(2,1)S(1)}, u32[]{:S(2)}, u32[]{:S(2)}) collective-permute-start(bf16[160,384]{1,0:T(8,128)(2,1)S(1)} %get-tuple-element.26), channel_id=1, source_target_pairs={{0,12},{4,0},{8,4},{12,8},{1,13},{5,1},{9,5},{13,9},{2,14},{6,2},{... | collective-permute-start | bytes 368648 | tf_op jit(solution)/shard_map/ppermute | solution.py:20
  146.2 4.0 %collective-permute-done.6 = bf16[160,384]{1,0:T(8,128)(2,1)S(1)} collective-permute-done((bf16[160,384]{1,0:T(8,128)(2,1)S(1)}, bf16[160,384]{1,0:T(8,128)(2,1)S(1)}, u32[]{:S(2)}, u32[]{:S(2)}) %collective-permute-start.6) | collective-permute-done | bytes 122912 | tf_op jit(solution)/shard_map/ppermute | solution.py:20
  150.2 1.5 collective-permute-done.8
  151.8 5.7 %collective-permute-start.7 = (bf16[320,384]{1,0:T(8,128)(2,1)S(1)}, bf16[320,384]{1,0:T(8,128)(2,1)S(1)}, u32[]{:S(2)}, u32[]{:S(2)}) collective-permute-start(bf16[320,384]{1,0:T(8,128)(2,1)S(1)} %pad_maximum_fusion.3), channel_id=1, source_target_pairs={{0,4},{4,8},{8,12},{12,0},{1,5},{5,9},{9,13},{13,1},{2,6},{6,10},{... | collective-permute-start | bytes 737288 | tf_op jit(solution)/shard_map/ppermute | solution.py:20
  157.5 3.5 %collective-permute-start.9 = (bf16[320,384]{1,0:T(8,128)(2,1)S(1)}, bf16[320,384]{1,0:T(8,128)(2,1)S(1)}, u32[]{:S(2)}, u32[]{:S(2)}) collective-permute-start(bf16[320,384]{1,0:T(8,128)(2,1)S(1)} %pad_maximum_fusion.4), channel_id=1, source_target_pairs={{0,12},{4,0},{8,4},{12,8},{1,13},{5,1},{9,5},{13,9},{2,14},{6,2},{... | collective-permute-start | bytes 737288 | tf_op jit(solution)/shard_map/ppermute | solution.py:20
  161.0 7.2 %collective-permute-done.7 = bf16[320,384]{1,0:T(8,128)(2,1)S(1)} collective-permute-done((bf16[320,384]{1,0:T(8,128)(2,1)S(1)}, bf16[320,384]{1,0:T(8,128)(2,1)S(1)}, u32[]{:S(2)}, u32[]{:S(2)}) %collective-permute-start.7) | collective-permute-done | bytes 245792 | tf_op jit(solution)/shard_map/ppermute | solution.py:20
  168.3 4.1 %collective-permute-done.9 = bf16[320,384]{1,0:T(8,128)(2,1)S(1)} collective-permute-done((bf16[320,384]{1,0:T(8,128)(2,1)S(1)}, bf16[320,384]{1,0:T(8,128)(2,1)S(1)}, u32[]{:S(2)}, u32[]{:S(2)}) %collective-permute-start.9) | collective-permute-done | bytes 245792 | tf_op jit(solution)/shard_map/ppermute | solution.py:20
  172.5 0.7 fusion.19
  173.1 0.7 fusion.17
  173.8 1.4 fusion.26
  175.2 26.3 %all-to-all-start.1 = ((bf16[64,16,128]{2,1,0:T(8,128)(2,1)}), bf16[64,16,128]{2,1,0:T(8,128)(2,1)S(1)}, u32[]{:S(2)}, u32[]{:S(2)}) async-start(bf16[64,16,128]{2,1,0:T(8,128)(2,1)} %bitcast.29), calls=%async_computation.1 | async-start | bytes 524288 | tf_op jit(solution)/shard_map/all_to_all | solution.py:115
  201.6 11.9 %all-to-all-done.1 = bf16[64,16,128]{2,1,0:T(8,128)(2,1)S(1)} async-done(((bf16[64,16,128]{2,1,0:T(8,128)(2,1)}), bf16[64,16,128]{2,1,0:T(8,128)(2,1)S(1)}, u32[]{:S(2)}, u32[]{:S(2)}) %all-to-all-start.1) | async-done | bytes 262176 | tf_op jit(solution)/shard_map/all_to_all | solution.py:115
  215.4 0.8 copy.7
  (43 shorter events, 2.9 us)
Async XLA Ops:
  0.0 120.1 %copy-start = (bf16[1,6144,128]{2,1,0:T(8,128)(2,1)S(1)}, bf16[1,6144,128]{2,1,0:T(8,128)(2,1)}, u32[]{:S(2)}) copy-start(bf16[1,6144,128]{2,1,0:T(8,128)(2,1)} %param.8) | copy-start | bytes 4718596
  0.0 7.4 %copy-start.5 = (s32[128,2]{0,1:T(2,128)S(1)}, s32[128,2]{0,1:T(2,128)}, u32[]{:S(2)}) copy-start(s32[128,2]{0,1:T(2,128)} %param.6) | copy-start | bytes 3076
  0.0 7.5 %copy-start.4 = (bf16[128,384]{1,0:T(8,128)(2,1)S(1)}, bf16[128,384]{1,0:T(8,128)(2,1)}, u32[]{:S(2)}) copy-start(bf16[128,384]{1,0:T(8,128)(2,1)} %param.5) | copy-start | bytes 294916
  2.5 122.6 %collective-permute-start.3 = (bf16[128,1536]{1,0:T(8,128)(2,1)S(1)}, bf16[128,1536]{1,0:T(8,128)(2,1)}, u32[]{:S(2)}, u32[]{:S(2)}) collective-permute-start(bf16[128,1536]{1,0:T(8,128)(2,1)S(1)} %pad_maximum_fusion), channel_id=1, source_target_pairs={{0,1},{1,0},{2,3},{3,2},{4,5},{5,4},{6,7},{7,6},{8,9},{9,8},{10,11... | collective-permute-start | bytes 1179656 | tf_op jit(solution)/shard_map/ppermute | solution.py:15
  9.6 27.2 %all-to-all-start = ((bf16[64,16,128]{2,1,0:T(8,128)(2,1)}), bf16[64,16,128]{2,1,0:T(8,128)(2,1)S(1)}, u32[]{:S(2)}, u32[]{:S(2)}) async-start(bf16[64,16,128]{2,1,0:T(8,128)(2,1)} %bitcast.10), calls=%async_computation | async-start | bytes 524288 | tf_op jit(solution)/shard_map/all_to_all | solution.py:71
  24.8 105.8 %collective-permute-start.4 = (bf16[128,1536]{1,0:T(8,128)(2,1)S(1)}, bf16[128,1536]{1,0:T(8,128)(2,1)}, u32[]{:S(2)}, u32[]{:S(2)}) collective-permute-start(bf16[128,1536]{1,0:T(8,128)(2,1)S(1)} %pad_maximum_fusion.1), channel_id=1, source_target_pairs={{0,2},{1,3},{2,0},{3,1},{4,6},{5,7},{6,4},{7,5},{8,10},{9,11},{10,... | collective-permute-start | bytes 1179656 | tf_op jit(solution)/shard_map/ppermute | solution.py:15
  26.8 103.8 %collective-permute-start.5 = (bf16[128,1536]{1,0:T(8,128)(2,1)S(1)}, bf16[128,1536]{1,0:T(8,128)(2,1)}, u32[]{:S(2)}, u32[]{:S(2)}) collective-permute-start(bf16[128,1536]{1,0:T(8,128)(2,1)S(1)} %pad_maximum_fusion.2), channel_id=1, source_target_pairs={{0,3},{1,2},{2,1},{3,0},{4,7},{5,6},{6,5},{7,4},{8,11},{9,10},{10,... | collective-permute-start | bytes 1179656 | tf_op jit(solution)/shard_map/ppermute | solution.py:15
  120.1 12.7 %copy-start.1 = (bf16[128,384]{1,0:T(8,128)(2,1)S(1)}, bf16[128,384]{1,0:T(8,128)(2,1)}, u32[]{:S(2)}) copy-start(bf16[128,384]{1,0:T(8,128)(2,1)} %get-tuple-element.20) | copy-start | bytes 294916
  120.1 12.7 %copy-start.2 = (bf16[128,384]{1,0:T(8,128)(2,1)S(1)}, bf16[128,384]{1,0:T(8,128)(2,1)}, u32[]{:S(2)}) copy-start(bf16[128,384]{1,0:T(8,128)(2,1)} %get-tuple-element.21) | copy-start | bytes 294916
  120.1 12.7 %copy-start.3 = (bf16[128,384]{1,0:T(8,128)(2,1)S(1)}, bf16[128,384]{1,0:T(8,128)(2,1)}, u32[]{:S(2)}) copy-start(bf16[128,384]{1,0:T(8,128)(2,1)} %get-tuple-element.22) | copy-start | bytes 294916
  121.3 9.3 %collective-permute-start = (bf16[320,128]{1,0:T(8,128)(2,1)S(1)}, bf16[320,128]{1,0:T(8,128)(2,1)S(1)}, u32[]{:S(2)}, u32[]{:S(2)}) collective-permute-start(bf16[320,128]{1,0:T(8,128)(2,1)S(1)} %multiply_convert_fusion), channel_id=1, source_target_pairs={{0,1},{1,0},{2,3},{3,2},{4,5},{5,4},{6,7},{7,6},{8,9},{9,8},{10,11... | collective-permute-start | bytes 245768 | tf_op jit(solution)/shard_map/ppermute | solution.py:15
  123.2 7.4 %collective-permute-start.1 = (bf16[320,128]{1,0:T(8,128)(2,1)S(1)}, bf16[320,128]{1,0:T(8,128)(2,1)S(1)}, u32[]{:S(2)}, u32[]{:S(2)}) collective-permute-start(bf16[320,128]{1,0:T(8,128)(2,1)S(1)} %multiply_convert_fusion), channel_id=1, source_target_pairs={{0,2},{1,3},{2,0},{3,1},{4,6},{5,7},{6,4},{7,5},{8,10},{9,11},{10,... | collective-permute-start | bytes 245768 | tf_op jit(solution)/shard_map/ppermute | solution.py:15
  125.2 7.6 %collective-permute-start.2 = (bf16[320,128]{1,0:T(8,128)(2,1)S(1)}, bf16[320,128]{1,0:T(8,128)(2,1)S(1)}, u32[]{:S(2)}, u32[]{:S(2)}) collective-permute-start(bf16[320,128]{1,0:T(8,128)(2,1)S(1)} %multiply_convert_fusion), channel_id=1, source_target_pairs={{0,3},{1,2},{2,1},{3,0},{4,7},{5,6},{6,5},{7,4},{8,11},{9,10},{10,... | collective-permute-start | bytes 245768 | tf_op jit(solution)/shard_map/ppermute | solution.py:15
  137.0 13.2 %collective-permute-start.6 = (bf16[160,384]{1,0:T(8,128)(2,1)S(1)}, bf16[160,384]{1,0:T(8,128)(2,1)S(1)}, u32[]{:S(2)}, u32[]{:S(2)}) collective-permute-start(bf16[160,384]{1,0:T(8,128)(2,1)S(1)} %get-tuple-element.25), channel_id=1, source_target_pairs={{0,4},{4,8},{8,12},{12,0},{1,5},{5,9},{9,13},{13,1},{2,6},{6,10},{... | collective-permute-start | bytes 368648 | tf_op jit(solution)/shard_map/ppermute | solution.py:20
  140.2 11.5 %collective-permute-start.8 = (bf16[160,384]{1,0:T(8,128)(2,1)S(1)}, bf16[160,384]{1,0:T(8,128)(2,1)S(1)}, u32[]{:S(2)}, u32[]{:S(2)}) collective-permute-start(bf16[160,384]{1,0:T(8,128)(2,1)S(1)} %get-tuple-element.26), channel_id=1, source_target_pairs={{0,12},{4,0},{8,4},{12,8},{1,13},{5,1},{9,5},{13,9},{2,14},{6,2},{... | collective-permute-start | bytes 368648 | tf_op jit(solution)/shard_map/ppermute | solution.py:20
  151.8 16.4 %collective-permute-start.7 = (bf16[320,384]{1,0:T(8,128)(2,1)S(1)}, bf16[320,384]{1,0:T(8,128)(2,1)S(1)}, u32[]{:S(2)}, u32[]{:S(2)}) collective-permute-start(bf16[320,384]{1,0:T(8,128)(2,1)S(1)} %pad_maximum_fusion.3), channel_id=1, source_target_pairs={{0,4},{4,8},{8,12},{12,0},{1,5},{5,9},{9,13},{13,1},{2,6},{6,10},{... | collective-permute-start | bytes 737288 | tf_op jit(solution)/shard_map/ppermute | solution.py:20
  157.5 14.8 %collective-permute-start.9 = (bf16[320,384]{1,0:T(8,128)(2,1)S(1)}, bf16[320,384]{1,0:T(8,128)(2,1)S(1)}, u32[]{:S(2)}, u32[]{:S(2)}) collective-permute-start(bf16[320,384]{1,0:T(8,128)(2,1)S(1)} %pad_maximum_fusion.4), channel_id=1, source_target_pairs={{0,12},{4,0},{8,4},{12,8},{1,13},{5,1},{9,5},{13,9},{2,14},{6,2},{... | collective-permute-start | bytes 737288 | tf_op jit(solution)/shard_map/ppermute | solution.py:20
  172.4 29.1 %copy-start.6 = (f32[128,2]{0,1:T(2,128)S(1)}, f32[128,2]{0,1:T(2,128)}, u32[]{:S(2)}) copy-start(f32[128,2]{0,1:T(2,128)} %param.7) | copy-start | bytes 3076
  175.2 38.3 %all-to-all-start.1 = ((bf16[64,16,128]{2,1,0:T(8,128)(2,1)}), bf16[64,16,128]{2,1,0:T(8,128)(2,1)S(1)}, u32[]{:S(2)}, u32[]{:S(2)}) async-start(bf16[64,16,128]{2,1,0:T(8,128)(2,1)} %bitcast.29), calls=%async_computation.1 | async-start | bytes 524288 | tf_op jit(solution)/shard_map/all_to_all | solution.py:115

commit v2 on v1

--- a/solution.py
+++ b/solution.py
@@ -60,13 +60,13 @@
     def chosen(pick, tile):
         return place[:, pick][:, None] + tile * capacity == spots
 
-    outgoing = jnp.zeros((experts * packed_rows, LANES), jnp.float32)
-    for tile in range(tiles):
-        both = (chosen(0, tile) | chosen(1, tile)).astype(jnp.bfloat16)
-        outgoing = outgoing + jnp.einsum(
-            "ts,tf->sf", both, tokens[:, tile * LANES : (tile + 1) * LANES],
-            preferred_element_type=jnp.float32,
-        )
+    both = jnp.concatenate([chosen(0, tile) | chosen(1, tile) for tile in range(tiles)], axis=0)
+    stacked = jnp.concatenate(
+        [tokens[:, tile * LANES : (tile + 1) * LANES] for tile in range(tiles)], axis=0
+    )
+    outgoing = jnp.einsum(
+        "ts,tf->sf", both.astype(jnp.bfloat16), stacked, preferred_element_type=jnp.float32
+    )
     outgoing = outgoing.astype(jnp.bfloat16).reshape(experts, packed_rows, LANES)
     received = lax.all_to_all(outgoing, "dp", split_axis=0, concat_axis=0, tiled=True)
     received = received.reshape(experts * packed_rows, LANES)
@@ -74,15 +74,11 @@
     rows = jnp.arange(row_count, dtype=jnp.int32)
     row_spot = (rows // capacity) * packed_rows + rows % capacity
 
-    def unpacker(tile):
-        return (row_spot[:, None] + tile * capacity == spots).astype(jnp.bfloat16)
-
+    row_spots = jnp.concatenate([row_spot + tile * capacity for tile in range(tiles)])
+    unpacker = (row_spots[:, None] == spots).astype(jnp.bfloat16)
+    flat_rows = jnp.dot(unpacker, received, preferred_element_type=jnp.float32)
     flat_rows = jnp.concatenate(
-        [
-            jnp.dot(unpacker(tile), received, preferred_element_type=jnp.float32)
-            for tile in range(tiles)
-        ],
-        axis=1,
+        [flat_rows[tile * row_count : (tile + 1) * row_count] for tile in range(tiles)], axis=1
     )
     scaled = (flat_rows * SCALE).astype(jnp.float16)
     gathered = lax.all_gather(scaled, ("hi", "lo"), axis=1, tiled=True)
@@ -91,38 +87,46 @@
     pieces = [hidden] + [swap(hidden, "lo", step) for step in range(1, low)]
     hidden = jnp.concatenate(pieces, axis=1)
     down_mine = jnp.concatenate(down_parts, axis=0)
-    part = jnp.dot(hidden, down_mine, preferred_element_type=jnp.float32)
 
-    keep, ahead, across, behind = [part[:, k * feat : (k + 1) * feat] for k in range(high)]
+    def block(k):
+        columns = down_mine[:, k * feat : (k + 1) * feat]
+        return jnp.dot(hidden, columns, preferred_element_type=jnp.float32)
+
     half = row_count // 2
-    across = across.astype(jnp.bfloat16)
-    from_behind = shift(across[:half], "hi", 1)
-    from_ahead = shift(across[half:], "hi", -1)
-    ahead = jnp.concatenate([ahead[:half] + from_behind.astype(jnp.float32), ahead[half:]], axis=0)
-    behind = jnp.concatenate([behind[:half], behind[half:] + from_ahead.astype(jnp.float32)], axis=0)
-    one = shift(ahead.astype(jnp.bfloat16), "hi", 1)
-    two = shift(behind.astype(jnp.bfloat16), "hi", -1)
-    result = keep + one.astype(jnp.float32) + two.astype(jnp.float32)
-    result = result.astype(jnp.bfloat16)
+    across = block(2).astype(jnp.bfloat16)
+    far_one = shift(across[:half], "hi", 1)
+    far_two = shift(across[half:], "hi", -1)
+    ahead, behind = block(1), block(3)
+    near_one = shift(ahead[half:].astype(jnp.bfloat16), "hi", 1)
+    near_two = shift(behind[:half].astype(jnp.bfloat16), "hi", -1)
+    keep = block(0)
+    sum_one = shift((ahead[:half] + far_one.astype(jnp.float32)).astype(jnp.bfloat16), "hi", 1)
+    sum_two = shift((behind[half:] + far_two.astype(jnp.float32)).astype(jnp.bfloat16), "hi", -1)
+    upper = keep[:half] + near_two.astype(jnp.float32) + sum_one.astype(jnp.float32)
+    lower = keep[half:] + near_one.astype(jnp.float32) + sum_two.astype(jnp.float32)
+    result = jnp.concatenate([upper, lower], axis=0).astype(jnp.bfloat16)
 
-    packed = jnp.zeros((experts * packed_rows, LANES), jnp.float32)
-    for tile in range(tiles):
-        packed = packed + jnp.einsum(
-            "rs,rf->sf", unpacker(tile), result[:, tile * LANES : (tile + 1) * LANES],
-            preferred_element_type=jnp.float32,
-        )
+    stacked = jnp.concatenate(
+        [result[:, tile * LANES : (tile + 1) * LANES] for tile in range(tiles)], axis=0
+    )
+    spot = jnp.arange(experts * packed_rows, dtype=jnp.int32)
+    within = spot % packed_rows
+    source_row = within // capacity * row_count + spot // packed_rows * capacity + within % capacity
+    source_row = jnp.where(within < tiles * capacity, source_row, -1)
+    packer = source_row[:, None] == jnp.arange(tiles * row_count, dtype=jnp.int32)[None, :]
+    packed = jnp.dot(packer.astype(jnp.bfloat16), stacked, preferred_element_type=jnp.float32)
     packed = packed.astype(jnp.bfloat16).reshape(experts, packed_rows, LANES)
     returned = lax.all_to_all(packed, "dp", split_axis=0, concat_axis=0, tiled=True)
     returned = returned.reshape(experts * packed_rows, LANES)
-    columns = []
-    for tile in range(tiles):
-        total = 0.0
-        for pick in range(picks):
-            one_hot = chosen(pick, tile).astype(jnp.bfloat16)
-            row = jnp.dot(one_hot, returned, preferred_element_type=jnp.float32)
-            total = total + row * combine[:, pick][:, None]
-        columns.append(total)
-    return jnp.concatenate(columns, axis=1).astype(jnp.bfloat16)
+    spread = jnp.concatenate(
+        [jnp.roll(returned, -tile * capacity, axis=0) for tile in range(tiles)], axis=1
+    )
+    total = 0.0
+    for pick in range(picks):
+        one_hot = chosen(pick, 0).astype(jnp.bfloat16)
+        row = jnp.dot(one_hot, spread, preferred_element_type=jnp.float32)
+        total = total + row * combine[:, pick][:, None]
+    return with_layout_constraint(total.astype(jnp.bfloat16), Layout(major_to_minor=(0, 1)))
 
 
 def solution(mesh):

time: 217 us -> 208 us (0.959)
  waiting for transfers between devices: 35.1 us -> 29.1 us
  other arithmetic: 0.55 us -> 5.55 us
  matrix products: 13.2 us -> 8.53 us
  starting transfers between devices: 81.6 us -> 77.7 us
    all_to_all x1, starting transfers between devices: 26.3 us -> 14.8 us  [on_device(): lax.all_to_all(packed, 'dp', split_axis=0, concat_axis=0, tiled=True)]
    ppermute x4 -> x6, starting transfers between devices: 18.4 us -> 25.4 us  [shift(): lax.ppermute(value, axis, [(i, (i + step) % size) for i in range(size)])]
    dot_general x16 -> x9, matrix products: 12 us -> 7.31 us  [the longest x1 1.72 us: on_device(): flat_rows = jnp.dot(unpacker, received, preferred_element_type=jnp.float32)]
    all_to_all x1, waiting for transfers between devices: 4.24 us -> 0.47 us  [on_device(): lax.all_to_all(outgoing, 'dp', split_axis=0, concat_axis=0, tiled=True)]
    all_to_all x1, starting transfers between devices: 15.2 us -> 18.9 us  [on_device(): lax.all_to_all(outgoing, 'dp', split_axis=0, concat_axis=0, tiled=True)]
    ppermute x6, starting transfers between devices: 21.7 us -> 18.5 us  [swap(): return lax.ppermute(value, axis, [(i, i ^ step) for i in range(size)])]
    concatenate x3, other arithmetic: 0.06 us -> 2.5 us  [the longest x1 2.41 us: on_device(): down_mine = jnp.concatenate(down_parts, axis=0)]
    dynamic_slice x1, local copies, waits for them, and re-layouts: 2.5 us -> 0.31 us  [share(): lax.dynamic_slice_in_dim(down_local, owner * feat, feat, axis=1)]
  transfers between devices with their start and end apart: 12 -> 14, of which waited for: 7 -> 5; matrix products, arithmetic and copies ran while one was open for 2% -> 4% of each run, Pallas kernels for 0% -> 0%
where the time goes in v2:
time: 208 us; the launch traced here: 207 us
  blocking collectives  83.6 us (40%)
  starting transfers between devices  77.7 us (37%)
  waiting for transfers between devices  29.1 us (14%)
  matrix products  8.53 us (4%)
  other arithmetic  5.55 us (3%)
  local copies, waits for them, and re-layouts  2.19 us (1%)
    all_gather x1, blocking collectives, on_device(): gathered = lax.all_gather(scaled, ('hi', 'lo'), axis=1, tiled=True)  83.6 us
    ppermute x6, starting transfers between devices, shift(): lax.ppermute(value, axis, [(i, (i + step) % size) for i in range(size)])  25.4 us
    all_to_all x1, starting transfers between devices, on_device(): lax.all_to_all(outgoing, 'dp', split_axis=0, concat_axis=0, tiled=True)  18.9 us
    ppermute x6, starting transfers between devices, swap(): return lax.ppermute(value, axis, [(i, i ^ step) for i in range(size)])  18.5 us
    ppermute x6, waiting for transfers between devices, shift(): lax.ppermute(value, axis, [(i, (i + step) % size) for i in range(size)])  16.7 us
    all_to_all x1, starting transfers between devices, on_device(): lax.all_to_all(packed, 'dp', split_axis=0, concat_axis=0, tiled=True)  14.8 us
    all_to_all x1, waiting for transfers between devices, on_device(): lax.all_to_all(packed, 'dp', split_axis=0, concat_axis=0, tiled=True)  12 us
  transfers between devices with their start and end apart: 14, of which 5 were waited for; matrix products, arithmetic and copies ran while one was open for 4% of the time, Pallas kernels for 0%

profile of v2, /device:TPU:1, one launch (start us, length us, event | category | flops | bytes accessed | tf_op | source)
XLA Modules:
  0.0 207.3 jit_solution(1206779536884733879)
XLA Ops:
  0.0 0.8 slice_bitcast_fusion.2
  0.9 0.7 add_add_fusion
  1.6 0.8 fusion.95
  2.9 1.3 fusion.13
  4.2 18.9 %all-to-all-start = ((bf16[64,16,128]{2,1,0:T(8,128)(2,1)}), bf16[64,16,128]{2,1,0:T(8,128)(2,1)}, u32[]{:S(2)}, u32[]{:S(2)}) async-start(bf16[64,16,128]{2,1,0:T(8,128)(2,1)} %bitcast.10), calls=%async_computation | async-start | bytes 524288 | tf_op jit(solution)/shard_map/all_to_all | solution.py:71
  23.7 1.9 collective-permute-start.3
  25.6 0.8 pad_maximum_fusion.2
  26.4 1.9 collective-permute-start.4
  28.3 0.8 pad_maximum_fusion.3
  29.1 5.4 %collective-permute-start.5 = (bf16[128,1536]{1,0:T(8,128)(2,1)}, bf16[128,1536]{1,0:T(8,128)(2,1)S(1)}, u32[]{:S(2)}, u32[]{:S(2)}) collective-permute-start(bf16[128,1536]{1,0:T(8,128)(2,1)} %pad_maximum_fusion.3), channel_id=1, source_target_pairs={{0,3},{1,2},{2,1},{3,0},{4,7},{5,6},{6,5},{7,4},{8,11},{9,10},{10,... | collective-permute-start | bytes 1179656 | tf_op jit(solution)/shard_map/ppermute | solution.py:15
  34.6 0.5 all-to-all-done
  35.1 1.7 fusion.3
  36.9 83.6 %all-gather.1 = f16[320,6144]{1,0:T(8,128)(2,1)S(1)} all-gather(f16[320,384]{1,0:T(8,128)(2,1)S(1)} %fusion.27), channel_id=1, replica_groups=mesh['dp'=64,'hi'=4,'lo'=4] {'hi','lo'}, dimensions={1}, use_global_device_ids=true | all-gather | bytes 4177920 | tf_op jit(solution)/shard_map/all_gather | solution.py:84
  120.5 1.2 multiply_convert_fusion
  121.7 1.9 collective-permute-start
  123.7 1.9 collective-permute-start.1
  125.6 5.4 %collective-permute-start.2 = (bf16[320,128]{1,0:T(8,128)(2,1)S(1)}, bf16[320,128]{1,0:T(8,128)(2,1)S(1)}, u32[]{:S(2)}, u32[]{:S(2)}) collective-permute-start(bf16[320,128]{1,0:T(8,128)(2,1)S(1)} %multiply_convert_fusion), channel_id=1, source_target_pairs={{0,3},{1,2},{2,1},{3,0},{4,7},{5,6},{6,5},{7,4},{8,11},{9,10},{10,... | collective-permute-start | bytes 245768 | tf_op jit(solution)/shard_map/ppermute | solution.py:15
  131.1 2.4 %pad_maximum_fusion = bf16[512,1536]{1,0:T(8,128)(2,1)S(1)} fusion(bf16[128,1536]{1,0:T(8,128)(2,1)S(1)} %collective-permute-done.5, bf16[128,1536]{1,0:T(8,128)(2,1)S(1)} %collective-permute-done.4, bf16[128,1536]{1,0:T(8,128)(2,1)S(1)} %collective-permute-done.3, bf16[128,384]{1,0:T(8,128)(2,1)S(1)} %get-tuple-element.18, ...), kind=kLoop, calls=%fused_computation.8 | loop fusion | flops 11010048 | bytes 3145728 | tf_op jit(solution)/shard_map/concatenate | solution.py:89
  133.9 4.2 %collective-permute-start.10 = (bf16[160,384]{1,0:T(8,128)(2,1)S(1)}, bf16[160,384]{1,0:T(8,128)(2,1)S(1)}, u32[]{:S(2)}, u32[]{:S(2)}) collective-permute-start(bf16[160,384]{1,0:T(8,128)(2,1)S(1)} %get-tuple-element.31), channel_id=1, source_target_pairs={{0,12},{4,0},{8,4},{12,8},{1,13},{5,1},{9,5},{13,9},{2,14},{6,2},{... | collective-permute-start | bytes 368648 | tf_op jit(solution)/shard_map/ppermute | solution.py:20
  138.5 4.6 %collective-permute-start.6 = (bf16[160,384]{1,0:T(8,128)(2,1)S(1)}, bf16[160,384]{1,0:T(8,128)(2,1)S(1)}, u32[]{:S(2)}, u32[]{:S(2)}) collective-permute-start(bf16[160,384]{1,0:T(8,128)(2,1)S(1)} %slice.214), channel_id=1, source_target_pairs={{0,12},{4,0},{8,4},{12,8},{1,13},{5,1},{9,5},{13,9},{2,14},{6,2},{... | collective-permute-start | bytes 368648 | tf_op jit(solution)/shard_map/ppermute | solution.py:20
  143.1 4.6 %collective-permute-start.7 = (bf16[160,384]{1,0:T(8,128)(2,1)S(1)}, bf16[160,384]{1,0:T(8,128)(2,1)S(1)}, u32[]{:S(2)}, u32[]{:S(2)}) collective-permute-start(bf16[160,384]{1,0:T(8,128)(2,1)S(1)} %get-tuple-element.30), channel_id=1, source_target_pairs={{0,4},{4,8},{8,12},{12,0},{1,5},{5,9},{9,13},{13,1},{2,6},{6,10},{... | collective-permute-start | bytes 368648 | tf_op jit(solution)/shard_map/ppermute | solution.py:20
  148.1 5.0 %collective-permute-start.9 = (bf16[160,384]{1,0:T(8,128)(2,1)S(1)}, bf16[160,384]{1,0:T(8,128)(2,1)S(1)}, u32[]{:S(2)}, u32[]{:S(2)}) collective-permute-start(bf16[160,384]{1,0:T(8,128)(2,1)S(1)} %slice.213), channel_id=1, source_target_pairs={{0,4},{4,8},{8,12},{12,0},{1,5},{5,9},{9,13},{13,1},{2,6},{6,10},{... | collective-permute-start | bytes 368648 | tf_op jit(solution)/shard_map/ppermute | solution.py:20
  153.1 4.2 %collective-permute-start.11 = (bf16[160,384]{1,0:T(8,128)(2,1)S(1)}, bf16[160,384]{1,0:T(8,128)(2,1)S(1)}, u32[]{:S(2)}, u32[]{:S(2)}) collective-permute-start(bf16[160,384]{1,0:T(8,128)(2,1)S(1)} %fusion.40), channel_id=1, source_target_pairs={{0,12},{4,0},{8,4},{12,8},{1,13},{5,1},{9,5},{13,9},{2,14},{6,2},{... | collective-permute-start | bytes 368648 | tf_op jit(solution)/shard_map/ppermute | solution.py:20
  157.3 2.1 %collective-permute-done.7 = bf16[160,384]{1,0:T(8,128)(2,1)S(1)} collective-permute-done((bf16[160,384]{1,0:T(8,128)(2,1)S(1)}, bf16[160,384]{1,0:T(8,128)(2,1)S(1)}, u32[]{:S(2)}, u32[]{:S(2)}) %collective-permute-start.7) | collective-permute-done | bytes 122912 | tf_op jit(solution)/shard_map/ppermute | solution.py:20
  159.5 2.8 %collective-permute-start.8 = (bf16[160,384]{1,0:T(8,128)(2,1)S(1)}, bf16[160,384]{1,0:T(8,128)(2,1)S(1)}, u32[]{:S(2)}, u32[]{:S(2)}) collective-permute-start(bf16[160,384]{1,0:T(8,128)(2,1)S(1)} %fusion.43), channel_id=1, source_target_pairs={{0,4},{4,8},{8,12},{12,0},{1,5},{5,9},{9,13},{13,1},{2,6},{6,10},{... | collective-permute-start | bytes 368648 | tf_op jit(solution)/shard_map/ppermute | solution.py:20
  162.7 5.6 %collective-permute-done.11 = bf16[160,384]{1,0:T(8,128)(2,1)S(1)} collective-permute-done((bf16[160,384]{1,0:T(8,128)(2,1)S(1)}, bf16[160,384]{1,0:T(8,128)(2,1)S(1)}, u32[]{:S(2)}, u32[]{:S(2)}) %collective-permute-start.11) | collective-permute-done | bytes 122912 | tf_op jit(solution)/shard_map/ppermute | solution.py:20
  168.3 8.9 %collective-permute-done.8 = bf16[160,384]{1,0:T(8,128)(2,1)S(1)} collective-permute-done((bf16[160,384]{1,0:T(8,128)(2,1)S(1)}, bf16[160,384]{1,0:T(8,128)(2,1)S(1)}, u32[]{:S(2)}, u32[]{:S(2)}) %collective-permute-start.8) | collective-permute-done | bytes 122912 | tf_op jit(solution)/shard_map/ppermute | solution.py:20
  177.4 1.6 fusion.16
  178.9 14.8 %all-to-all-start.1 = ((bf16[64,16,128]{2,1,0:T(8,128)(2,1)}), bf16[64,16,128]{2,1,0:T(8,128)(2,1)S(1)}, u32[]{:S(2)}, u32[]{:S(2)}) async-start(bf16[64,16,128]{2,1,0:T(8,128)(2,1)} %bitcast.29), calls=%async_computation.1 | async-start | bytes 524288 | tf_op jit(solution)/shard_map/all_to_all | solution.py:119
  193.7 12.0 %all-to-all-done.1 = bf16[64,16,128]{2,1,0:T(8,128)(2,1)S(1)} async-done(((bf16[64,16,128]{2,1,0:T(8,128)(2,1)}), bf16[64,16,128]{2,1,0:T(8,128)(2,1)S(1)}, u32[]{:S(2)}, u32[]{:S(2)}) %all-to-all-start.1) | async-done | bytes 262176 | tf_op jit(solution)/shard_map/all_to_all | solution.py:119
  205.9 0.4 convolution_multiply_fusion
  206.2 1.0 fusion.18
  (43 shorter events, 2.9 us)
Async XLA Ops:
  0.0 120.5 %copy-start = (bf16[1,6144,128]{2,1,0:T(8,128)(2,1)S(1)}, bf16[1,6144,128]{2,1,0:T(8,128)(2,1)}, u32[]{:S(2)}) copy-start(bf16[1,6144,128]{2,1,0:T(8,128)(2,1)} %param.8) | copy-start | bytes 4718596
  2.9 20.4 %copy-start.1 = (bf16[1,128,6144]{2,1,0:T(8,128)(2,1)S(1)}, bf16[1,128,6144]{2,1,0:T(8,128)(2,1)}, u32[]{:S(2)}) copy-start(bf16[1,128,6144]{2,1,0:T(8,128)(2,1)} %param.9) | copy-start | bytes 4718596
  4.2 30.9 %all-to-all-start = ((bf16[64,16,128]{2,1,0:T(8,128)(2,1)}), bf16[64,16,128]{2,1,0:T(8,128)(2,1)}, u32[]{:S(2)}, u32[]{:S(2)}) async-start(bf16[64,16,128]{2,1,0:T(8,128)(2,1)} %bitcast.10), calls=%async_computation | async-start | bytes 524288 | tf_op jit(solution)/shard_map/all_to_all | solution.py:71
  23.7 101.9 %collective-permute-start.3 = (bf16[128,1536]{1,0:T(8,128)(2,1)S(1)}, bf16[128,1536]{1,0:T(8,128)(2,1)S(1)}, u32[]{:S(2)}, u32[]{:S(2)}) collective-permute-start(bf16[128,1536]{1,0:T(8,128)(2,1)S(1)} %pad_maximum_fusion.1), channel_id=1, source_target_pairs={{0,1},{1,0},{2,3},{3,2},{4,5},{5,4},{6,7},{7,6},{8,9},{9,8},{10,11... | collective-permute-start | bytes 1179656 | tf_op jit(solution)/shard_map/ppermute | solution.py:15
  26.4 104.7 %collective-permute-start.4 = (bf16[128,1536]{1,0:T(8,128)(2,1)}, bf16[128,1536]{1,0:T(8,128)(2,1)S(1)}, u32[]{:S(2)}, u32[]{:S(2)}) collective-permute-start(bf16[128,1536]{1,0:T(8,128)(2,1)} %pad_maximum_fusion.2), channel_id=1, source_target_pairs={{0,2},{1,3},{2,0},{3,1},{4,6},{5,7},{6,4},{7,5},{8,10},{9,11},{10,... | collective-permute-start | bytes 1179656 | tf_op jit(solution)/shard_map/ppermute | solution.py:15
  29.1 102.0 %collective-permute-start.5 = (bf16[128,1536]{1,0:T(8,128)(2,1)}, bf16[128,1536]{1,0:T(8,128)(2,1)S(1)}, u32[]{:S(2)}, u32[]{:S(2)}) collective-permute-start(bf16[128,1536]{1,0:T(8,128)(2,1)} %pad_maximum_fusion.3), channel_id=1, source_target_pairs={{0,3},{1,2},{2,1},{3,0},{4,7},{5,6},{6,5},{7,4},{8,11},{9,10},{10,... | collective-permute-start | bytes 1179656 | tf_op jit(solution)/shard_map/ppermute | solution.py:15
  121.7 11.7 %collective-permute-start = (bf16[320,128]{1,0:T(8,128)(2,1)S(1)}, bf16[320,128]{1,0:T(8,128)(2,1)S(1)}, u32[]{:S(2)}, u32[]{:S(2)}) collective-permute-start(bf16[320,128]{1,0:T(8,128)(2,1)S(1)} %multiply_convert_fusion), channel_id=1, source_target_pairs={{0,1},{1,0},{2,3},{3,2},{4,5},{5,4},{6,7},{7,6},{8,9},{9,8},{10,11... | collective-permute-start | bytes 245768 | tf_op jit(solution)/shard_map/ppermute | solution.py:15
  123.7 9.8 %collective-permute-start.1 = (bf16[320,128]{1,0:T(8,128)(2,1)S(1)}, bf16[320,128]{1,0:T(8,128)(2,1)S(1)}, u32[]{:S(2)}, u32[]{:S(2)}) collective-permute-start(bf16[320,128]{1,0:T(8,128)(2,1)S(1)} %multiply_convert_fusion), channel_id=1, source_target_pairs={{0,2},{1,3},{2,0},{3,1},{4,6},{5,7},{6,4},{7,5},{8,10},{9,11},{10,... | collective-permute-start | bytes 245768 | tf_op jit(solution)/shard_map/ppermute | solution.py:15
  125.6 7.9 %collective-permute-start.2 = (bf16[320,128]{1,0:T(8,128)(2,1)S(1)}, bf16[320,128]{1,0:T(8,128)(2,1)S(1)}, u32[]{:S(2)}, u32[]{:S(2)}) collective-permute-start(bf16[320,128]{1,0:T(8,128)(2,1)S(1)} %multiply_convert_fusion), channel_id=1, source_target_pairs={{0,3},{1,2},{2,1},{3,0},{4,7},{5,6},{6,5},{7,4},{8,11},{9,10},{10,... | collective-permute-start | bytes 245768 | tf_op jit(solution)/shard_map/ppermute | solution.py:15
  133.9 19.2 %collective-permute-start.10 = (bf16[160,384]{1,0:T(8,128)(2,1)S(1)}, bf16[160,384]{1,0:T(8,128)(2,1)S(1)}, u32[]{:S(2)}, u32[]{:S(2)}) collective-permute-start(bf16[160,384]{1,0:T(8,128)(2,1)S(1)} %get-tuple-element.31), channel_id=1, source_target_pairs={{0,12},{4,0},{8,4},{12,8},{1,13},{5,1},{9,5},{13,9},{2,14},{6,2},{... | collective-permute-start | bytes 368648 | tf_op jit(solution)/shard_map/ppermute | solution.py:20
  138.5 24.2 %collective-permute-start.6 = (bf16[160,384]{1,0:T(8,128)(2,1)S(1)}, bf16[160,384]{1,0:T(8,128)(2,1)S(1)}, u32[]{:S(2)}, u32[]{:S(2)}) collective-permute-start(bf16[160,384]{1,0:T(8,128)(2,1)S(1)} %slice.214), channel_id=1, source_target_pairs={{0,12},{4,0},{8,4},{12,8},{1,13},{5,1},{9,5},{13,9},{2,14},{6,2},{... | collective-permute-start | bytes 368648 | tf_op jit(solution)/shard_map/ppermute | solution.py:20
  143.1 16.4 %collective-permute-start.7 = (bf16[160,384]{1,0:T(8,128)(2,1)S(1)}, bf16[160,384]{1,0:T(8,128)(2,1)S(1)}, u32[]{:S(2)}, u32[]{:S(2)}) collective-permute-start(bf16[160,384]{1,0:T(8,128)(2,1)S(1)} %get-tuple-element.30), channel_id=1, source_target_pairs={{0,4},{4,8},{8,12},{12,0},{1,5},{5,9},{9,13},{13,1},{2,6},{6,10},{... | collective-permute-start | bytes 368648 | tf_op jit(solution)/shard_map/ppermute | solution.py:20
  148.1 14.6 %collective-permute-start.9 = (bf16[160,384]{1,0:T(8,128)(2,1)S(1)}, bf16[160,384]{1,0:T(8,128)(2,1)S(1)}, u32[]{:S(2)}, u32[]{:S(2)}) collective-permute-start(bf16[160,384]{1,0:T(8,128)(2,1)S(1)} %slice.213), channel_id=1, source_target_pairs={{0,4},{4,8},{8,12},{12,0},{1,5},{5,9},{9,13},{13,1},{2,6},{6,10},{... | collective-permute-start | bytes 368648 | tf_op jit(solution)/shard_map/ppermute | solution.py:20
  153.1 15.3 %collective-permute-start.11 = (bf16[160,384]{1,0:T(8,128)(2,1)S(1)}, bf16[160,384]{1,0:T(8,128)(2,1)S(1)}, u32[]{:S(2)}, u32[]{:S(2)}) collective-permute-start(bf16[160,384]{1,0:T(8,128)(2,1)S(1)} %fusion.40), channel_id=1, source_target_pairs={{0,12},{4,0},{8,4},{12,8},{1,13},{5,1},{9,5},{13,9},{2,14},{6,2},{... | collective-permute-start | bytes 368648 | tf_op jit(solution)/shard_map/ppermute | solution.py:20
  159.5 17.7 %collective-permute-start.8 = (bf16[160,384]{1,0:T(8,128)(2,1)S(1)}, bf16[160,384]{1,0:T(8,128)(2,1)S(1)}, u32[]{:S(2)}, u32[]{:S(2)}) collective-permute-start(bf16[160,384]{1,0:T(8,128)(2,1)S(1)} %fusion.43), channel_id=1, source_target_pairs={{0,4},{4,8},{8,12},{12,0},{1,5},{5,9},{9,13},{13,1},{2,6},{6,10},{... | collective-permute-start | bytes 368648 | tf_op jit(solution)/shard_map/ppermute | solution.py:20
  177.3 16.4 %copy-start.2 = (f32[128,2]{0,1:T(2,128)S(1)}, f32[128,2]{0,1:T(2,128)}, u32[]{:S(2)}) copy-start(f32[128,2]{0,1:T(2,128)} %param.7) | copy-start | bytes 3076
  178.9 26.8 %all-to-all-start.1 = ((bf16[64,16,128]{2,1,0:T(8,128)(2,1)}), bf16[64,16,128]{2,1,0:T(8,128)(2,1)S(1)}, u32[]{:S(2)}, u32[]{:S(2)}) async-start(bf16[64,16,128]{2,1,0:T(8,128)(2,1)} %bitcast.29), calls=%async_computation.1 | async-start | bytes 524288 | tf_op jit(solution)/shard_map/all_to_all | solution.py:119

commit v3 on v2

--- a/solution.py
+++ b/solution.py
@@ -88,23 +88,30 @@
     hidden = jnp.concatenate(pieces, axis=1)
     down_mine = jnp.concatenate(down_parts, axis=0)
 
-    def block(k):
-        columns = down_mine[:, k * feat : (k + 1) * feat]
-        return jnp.dot(hidden, columns, preferred_element_type=jnp.float32)
+    half, reach = row_count // 2, high // 2
+    halves = [hidden[:half], hidden[half:]]
 
-    half = row_count // 2
-    across = block(2).astype(jnp.bfloat16)
-    far_one = shift(across[:half], "hi", 1)
-    far_two = shift(across[half:], "hi", -1)
-    ahead, behind = block(1), block(3)
-    near_one = shift(ahead[half:].astype(jnp.bfloat16), "hi", 1)
-    near_two = shift(behind[:half].astype(jnp.bfloat16), "hi", -1)
-    keep = block(0)
-    sum_one = shift((ahead[:half] + far_one.astype(jnp.float32)).astype(jnp.bfloat16), "hi", 1)
-    sum_two = shift((behind[half:] + far_two.astype(jnp.float32)).astype(jnp.bfloat16), "hi", -1)
-    upper = keep[:half] + near_two.astype(jnp.float32) + sum_one.astype(jnp.float32)
-    lower = keep[half:] + near_one.astype(jnp.float32) + sum_two.astype(jnp.float32)
-    result = jnp.concatenate([upper, lower], axis=0).astype(jnp.bfloat16)
+    def cut(k, part):
+        columns = down_mine[:, k % high * feat : (k % high + 1) * feat]
+        return jnp.dot(halves[part], columns, preferred_element_type=jnp.float32)
+
+    chains = [(0, 1, reach), (1, -1, reach), (1, 1, reach - 1), (0, -1, reach - 1)]
+    arrived = [None] * len(chains)
+    for distance in range(reach, 0, -1):
+        for number, (part, way, length) in enumerate(chains):
+            if distance <= length:
+                value = cut(way * distance, part)
+                if arrived[number] is not None:
+                    value = value + arrived[number].astype(jnp.float32)
+                arrived[number] = shift(value.astype(jnp.bfloat16), "hi", way)
+    sums = []
+    for part in range(2):
+        value = cut(0, part)
+        for number, chain in enumerate(chains):
+            if chain[0] == part:
+                value = value + arrived[number].astype(jnp.float32)
+        sums.append(value)
+    result = jnp.concatenate(sums, axis=0).astype(jnp.bfloat16)
 
     stacked = jnp.concatenate(
         [result[:, tile * LANES : (tile + 1) * LANES] for tile in range(tiles)], axis=0
@@ -131,7 +138,7 @@
 
 def solution(mesh):
     shape = mesh.devices.shape
-    low = 4
+    low = 2
     split = Mesh(mesh.devices.reshape(shape[0], shape[1] // low, low), ("dp", "hi", "lo"))
     tensor = ("hi", "lo")
     placed = (

time: 208 us -> 213 us (1.024)
  local copies, waits for them, and re-layouts: 2.19 us -> 14.8 us
  blocking collectives: 83.6 us -> 73.9 us
  starting transfers between devices: 77.7 us -> 85.4 us
  waiting for transfers between devices: 29.1 us -> 25 us
  other arithmetic: 5.55 us -> 1.58 us
    ppermute x6 -> x14, starting transfers between devices: 25.4 us -> 45.8 us  [shift(): lax.ppermute(value, axis, [(i, (i + step) % size) for i in range(size)])]
    ppermute x6 -> x2, starting transfers between devices: 18.5 us -> 4.18 us  [swap(): return lax.ppermute(value, axis, [(i, i ^ step) for i in range(size)])]
    unnamed x6 -> x11, local copies, waits for them, and re-layouts: 0.02 us -> 11.4 us
    all_gather x1, blocking collectives: 83.6 us -> 73.9 us  [on_device(): gathered = lax.all_gather(scaled, ('hi', 'lo'), axis=1, tiled=True)]
    ppermute x6 -> x14, waiting for transfers between devices: 16.7 us -> 10.2 us  [shift(): lax.ppermute(value, axis, [(i, (i + step) % size) for i in range(size)])]
    ppermute x6 -> x2, waiting for transfers between devices: 0.02 us -> 2.89 us  [swap(): return lax.ppermute(value, axis, [(i, i ^ step) for i in range(size)])]
    all_to_all x1, starting transfers between devices: 14.8 us -> 17.2 us  [on_device(): lax.all_to_all(packed, 'dp', split_axis=0, concat_axis=0, tiled=True)]
    concatenate x1, other arithmetic: 2.41 us -> 0.15 us  [on_device(): down_mine = jnp.concatenate(down_parts, axis=0)]
  transfers between devices with their start and end apart: 14 -> 18, of which waited for: 5 -> 5; matrix products, arithmetic and copies ran while one was open for 4% -> 9% of each run, Pallas kernels for 0% -> 0%
where the time goes in v3:
time: 213 us; the launch traced here: 211 us
  starting transfers between devices  85.4 us (40%)
  blocking collectives  73.9 us (35%)
  waiting for transfers between devices  25 us (12%)
  local copies, waits for them, and re-layouts  14.8 us (7%)
  matrix products  9.34 us (4%)
    all_gather x1, blocking collectives, on_device(): gathered = lax.all_gather(scaled, ('hi', 'lo'), axis=1, tiled=True)  73.9 us
    ppermute x14, starting transfers between devices, shift(): lax.ppermute(value, axis, [(i, (i + step) % size) for i in range(size)])  45.8 us
    all_to_all x1, starting transfers between devices, on_device(): lax.all_to_all(outgoing, 'dp', split_axis=0, concat_axis=0, tiled=True)  18.2 us
    all_to_all x1, starting transfers between devices, on_device(): lax.all_to_all(packed, 'dp', split_axis=0, concat_axis=0, tiled=True)  17.2 us
    all_to_all x1, waiting for transfers between devices, on_device(): lax.all_to_all(packed, 'dp', split_axis=0, concat_axis=0, tiled=True)  11.9 us
    unnamed x11, local copies, waits for them, and re-layouts  11.4 us
    ppermute x14, waiting for transfers between devices, shift(): lax.ppermute(value, axis, [(i, (i + step) % size) for i in range(size)])  10.2 us
  transfers between devices with their start and end apart: 18, of which 5 were waited for; matrix products, arithmetic and copies ran while one was open for 9% of the time, Pallas kernels for 0%

profile of v3, /device:TPU:1, one launch (start us, length us, event | category | flops | bytes accessed | tf_op | source)
XLA Modules:
  0.0 210.6 jit_solution(10144927987020632755)
XLA Ops:
  4.2 18.2 %all-to-all-start = ((bf16[64,16,128]{2,1,0:T(8,128)(2,1)}), bf16[64,16,128]{2,1,0:T(8,128)(2,1)S(1)}, u32[]{:S(2)}, u32[]{:S(2)}) async-start(bf16[64,16,128]{2,1,0:T(8,128)(2,1)} %bitcast.10), calls=%async_computation | async-start | bytes 524288 | tf_op jit(solution)/shard_map/all_to_all | solution.py:71
  22.6 1.6 bitcast_dynamic-update-slice_fusion.7
  24.2 1.6 bitcast_dynamic-update-slice_fusion.6
  25.8 1.6 bitcast_dynamic-update-slice_fusion.5
  27.5 1.6 bitcast_dynamic-update-slice_fusion.4
  29.1 1.6 bitcast_dynamic-update-slice_fusion.3
  30.7 1.6 bitcast_dynamic-update-slice_fusion.2
  32.3 1.6 bitcast_dynamic-update-slice_fusion.1
  34.0 1.6 bitcast_dynamic-update-slice_fusion
  35.6 1.9 collective-permute-start.1
  38.5 73.9 %all-gather.1 = f16[320,6144]{1,0:T(8,128)(2,1)S(1)} all-gather(f16[320,384]{1,0:T(8,128)(2,1)S(1)} %fusion.41), channel_id=1, replica_groups=mesh['dp'=64,'hi'=8,'lo'=2] {'hi','lo'}, dimensions={1}, use_global_device_ids=true | all-gather | bytes 4177920 | tf_op jit(solution)/shard_map/all_gather | solution.py:84
  113.6 2.3 %collective-permute-start = (bf16[320,128]{1,0:T(8,128)(2,1)S(1)}, bf16[320,128]{1,0:T(8,128)(2,1)S(1)}, u32[]{:S(2)}, u32[]{:S(2)}) collective-permute-start(bf16[320,128]{1,0:T(8,128)(2,1)S(1)} %multiply_convert_fusion), channel_id=1, source_target_pairs={{0,1},{1,0},{2,3},{3,2},{4,5},{5,4},{6,7},{7,6},{8,9},{9,8},{10,11... | collective-permute-start | bytes 245768 | tf_op jit(solution)/shard_map/ppermute | solution.py:15
  115.9 2.9 %collective-permute-done = bf16[320,128]{1,0:T(8,128)(2,1)S(1)} collective-permute-done((bf16[320,128]{1,0:T(8,128)(2,1)S(1)}, bf16[320,128]{1,0:T(8,128)(2,1)S(1)}, u32[]{:S(2)}, u32[]{:S(2)}) %collective-permute-start) | collective-permute-done | bytes 81952 | tf_op jit(solution)/shard_map/ppermute | solution.py:15
  119.2 1.9 collective-permute-start.13
  121.3 5.5 %collective-permute-start.9 = (bf16[160,384]{1,0:T(8,128)(2,1)S(1)}, bf16[160,384]{1,0:T(8,128)(2,1)S(1)}, u32[]{:S(2)}, u32[]{:S(2)}) collective-permute-start(bf16[160,384]{1,0:T(8,128)(2,1)S(1)} %convolution_convert_fusion.1), channel_id=1, source_target_pairs={{0,14},{2,0},{4,2},{6,4},{8,6},{10,8},{12,10},{14,12},{1,15},{3,1}... | collective-permute-start | bytes 368648 | tf_op jit(solution)/shard_map/ppermute | solution.py:20
  127.0 1.9 collective-permute-start.6
  129.1 4.3 %collective-permute-start.2 = (bf16[160,384]{1,0:T(8,128)(2,1)S(1)}, bf16[160,384]{1,0:T(8,128)(2,1)S(1)}, u32[]{:S(2)}, u32[]{:S(2)}) collective-permute-start(bf16[160,384]{1,0:T(8,128)(2,1)S(1)} %convolution_convert_fusion.3), channel_id=1, source_target_pairs={{0,2},{2,4},{4,6},{6,8},{8,10},{10,12},{12,14},{14,0},{1,3},{3,5},... | collective-permute-start | bytes 368648 | tf_op jit(solution)/shard_map/ppermute | solution.py:20
  133.6 1.9 collective-permute-start.14
  135.7 5.5 %collective-permute-start.10 = (bf16[160,384]{1,0:T(8,128)(2,1)S(1)}, bf16[160,384]{1,0:T(8,128)(2,1)S(1)}, u32[]{:S(2)}, u32[]{:S(2)}) collective-permute-start(bf16[160,384]{1,0:T(8,128)(2,1)S(1)} %fusion.29), channel_id=1, source_target_pairs={{0,14},{2,0},{4,2},{6,4},{8,6},{10,8},{12,10},{14,12},{1,15},{3,1}... | collective-permute-start | bytes 368648 | tf_op jit(solution)/shard_map/ppermute | solution.py:20
  141.4 1.9 collective-permute-start.7
  143.6 4.3 %collective-permute-start.3 = (bf16[160,384]{1,0:T(8,128)(2,1)S(1)}, bf16[160,384]{1,0:T(8,128)(2,1)S(1)}, u32[]{:S(2)}, u32[]{:S(2)}) collective-permute-start(bf16[160,384]{1,0:T(8,128)(2,1)S(1)} %fusion.23), channel_id=1, source_target_pairs={{0,2},{2,4},{4,6},{6,8},{8,10},{10,12},{12,14},{14,0},{1,3},{3,5},... | collective-permute-start | bytes 368648 | tf_op jit(solution)/shard_map/ppermute | solution.py:20
  148.1 1.9 collective-permute-start.15
  150.2 5.5 %collective-permute-start.11 = (bf16[160,384]{1,0:T(8,128)(2,1)S(1)}, bf16[160,384]{1,0:T(8,128)(2,1)S(1)}, u32[]{:S(2)}, u32[]{:S(2)}) collective-permute-start(bf16[160,384]{1,0:T(8,128)(2,1)S(1)} %fusion.28), channel_id=1, source_target_pairs={{0,14},{2,0},{4,2},{6,4},{8,6},{10,8},{12,10},{14,12},{1,15},{3,1}... | collective-permute-start | bytes 368648 | tf_op jit(solution)/shard_map/ppermute | solution.py:20
  155.9 1.9 collective-permute-start.8
  158.0 4.3 %collective-permute-start.4 = (bf16[160,384]{1,0:T(8,128)(2,1)S(1)}, bf16[160,384]{1,0:T(8,128)(2,1)S(1)}, u32[]{:S(2)}, u32[]{:S(2)}) collective-permute-start(bf16[160,384]{1,0:T(8,128)(2,1)S(1)} %fusion.22), channel_id=1, source_target_pairs={{0,2},{2,4},{4,6},{6,8},{8,10},{10,12},{12,14},{14,0},{1,3},{3,5},... | collective-permute-start | bytes 368648 | tf_op jit(solution)/shard_map/ppermute | solution.py:20
  162.5 3.1 %collective-permute-start.12 = (bf16[160,384]{1,0:T(8,128)(2,1)S(1)}, bf16[160,384]{1,0:T(8,128)(2,1)S(1)}, u32[]{:S(2)}, u32[]{:S(2)}) collective-permute-start(bf16[160,384]{1,0:T(8,128)(2,1)S(1)} %fusion.27), channel_id=1, source_target_pairs={{0,14},{2,0},{4,2},{6,4},{8,6},{10,8},{12,10},{14,12},{1,15},{3,1}... | collective-permute-start | bytes 368648 | tf_op jit(solution)/shard_map/ppermute | solution.py:20
  165.6 3.1 %collective-permute-done.4 = bf16[160,384]{1,0:T(8,128)(2,1)S(1)} collective-permute-done((bf16[160,384]{1,0:T(8,128)(2,1)S(1)}, bf16[160,384]{1,0:T(8,128)(2,1)S(1)}, u32[]{:S(2)}, u32[]{:S(2)}) %collective-permute-start.4) | collective-permute-done | bytes 122912 | tf_op jit(solution)/shard_map/ppermute | solution.py:20
  168.9 1.9 collective-permute-start.5
  172.3 5.8 %collective-permute-done.5 = bf16[160,384]{1,0:T(8,128)(2,1)S(1)} collective-permute-done((bf16[160,384]{1,0:T(8,128)(2,1)S(1)}, bf16[160,384]{1,0:T(8,128)(2,1)S(1)}, u32[]{:S(2)}, u32[]{:S(2)}) %collective-permute-start.5) | collective-permute-done | bytes 122912 | tf_op jit(solution)/shard_map/ppermute | solution.py:20
  178.3 1.5 fusion.16
  179.9 17.2 %all-to-all-start.1 = ((bf16[64,16,128]{2,1,0:T(8,128)(2,1)}), bf16[64,16,128]{2,1,0:T(8,128)(2,1)S(1)}, u32[]{:S(2)}, u32[]{:S(2)}) async-start(bf16[64,16,128]{2,1,0:T(8,128)(2,1)} %bitcast.29), calls=%async_computation.1 | async-start | bytes 524288 | tf_op jit(solution)/shard_map/all_to_all | solution.py:126
  197.2 11.9 %all-to-all-done.1 = bf16[64,16,128]{2,1,0:T(8,128)(2,1)S(1)} async-done(((bf16[64,16,128]{2,1,0:T(8,128)(2,1)}), bf16[64,16,128]{2,1,0:T(8,128)(2,1)S(1)}, u32[]{:S(2)}, u32[]{:S(2)}) %all-to-all-start.1) | async-done | bytes 262176 | tf_op jit(solution)/shard_map/all_to_all | solution.py:126
  (60 shorter events, 12.5 us)
Async XLA Ops:
  0.0 112.4 %copy-start = (bf16[1,6144,128]{2,1,0:T(8,128)(2,1)S(1)}, bf16[1,6144,128]{2,1,0:T(8,128)(2,1)}, u32[]{:S(2)}) copy-start(bf16[1,6144,128]{2,1,0:T(8,128)(2,1)} %param.8) | copy-start | bytes 4718596
  4.2 33.4 %all-to-all-start = ((bf16[64,16,128]{2,1,0:T(8,128)(2,1)}), bf16[64,16,128]{2,1,0:T(8,128)(2,1)S(1)}, u32[]{:S(2)}, u32[]{:S(2)}) async-start(bf16[64,16,128]{2,1,0:T(8,128)(2,1)} %bitcast.10), calls=%async_computation | async-start | bytes 524288 | tf_op jit(solution)/shard_map/all_to_all | solution.py:71
  35.6 83.3 %collective-permute-start.1 = (bf16[128,3072]{1,0:T(8,128)(2,1)}, bf16[128,3072]{1,0:T(8,128)(2,1)S(1)}, u32[]{:S(2)}, u32[]{:S(2)}) collective-permute-start(bf16[128,3072]{1,0:T(8,128)(2,1)} %get-tuple-element.14), channel_id=1, source_target_pairs={{0,1},{1,0},{2,3},{3,2},{4,5},{5,4},{6,7},{7,6},{8,9},{9,8},{10,11... | collective-permute-start | bytes 2359304 | tf_op jit(solution)/shard_map/ppermute | solution.py:15
  113.6 5.2 %collective-permute-start = (bf16[320,128]{1,0:T(8,128)(2,1)S(1)}, bf16[320,128]{1,0:T(8,128)(2,1)S(1)}, u32[]{:S(2)}, u32[]{:S(2)}) collective-permute-start(bf16[320,128]{1,0:T(8,128)(2,1)S(1)} %multiply_convert_fusion), channel_id=1, source_target_pairs={{0,1},{1,0},{2,3},{3,2},{4,5},{5,4},{6,7},{7,6},{8,9},{9,8},{10,11... | collective-permute-start | bytes 245768 | tf_op jit(solution)/shard_map/ppermute | solution.py:15
  119.2 14.2 %collective-permute-start.13 = (bf16[160,384]{1,0:T(8,128)(2,1)S(1)}, bf16[160,384]{1,0:T(8,128)(2,1)S(1)}, u32[]{:S(2)}, u32[]{:S(2)}) collective-permute-start(bf16[160,384]{1,0:T(8,128)(2,1)S(1)} %convolution_convert_fusion), channel_id=1, source_target_pairs={{0,2},{2,4},{4,6},{6,8},{8,10},{10,12},{12,14},{14,0},{1,3},{3,5},... | collective-permute-start | bytes 368648 | tf_op jit(solution)/shard_map/ppermute | solution.py:20
  121.3 14.2 %collective-permute-start.9 = (bf16[160,384]{1,0:T(8,128)(2,1)S(1)}, bf16[160,384]{1,0:T(8,128)(2,1)S(1)}, u32[]{:S(2)}, u32[]{:S(2)}) collective-permute-start(bf16[160,384]{1,0:T(8,128)(2,1)S(1)} %convolution_convert_fusion.1), channel_id=1, source_target_pairs={{0,14},{2,0},{4,2},{6,4},{8,6},{10,8},{12,10},{14,12},{1,15},{3,1}... | collective-permute-start | bytes 368648 | tf_op jit(solution)/shard_map/ppermute | solution.py:20
  127.0 14.2 %collective-permute-start.6 = (bf16[160,384]{1,0:T(8,128)(2,1)S(1)}, bf16[160,384]{1,0:T(8,128)(2,1)S(1)}, u32[]{:S(2)}, u32[]{:S(2)}) collective-permute-start(bf16[160,384]{1,0:T(8,128)(2,1)S(1)} %convolution_convert_fusion.2), channel_id=1, source_target_pairs={{0,14},{2,0},{4,2},{6,4},{8,6},{10,8},{12,10},{14,12},{1,15},{3,1}... | collective-permute-start | bytes 368648 | tf_op jit(solution)/shard_map/ppermute | solution.py:20
  129.1 14.2 %collective-permute-start.2 = (bf16[160,384]{1,0:T(8,128)(2,1)S(1)}, bf16[160,384]{1,0:T(8,128)(2,1)S(1)}, u32[]{:S(2)}, u32[]{:S(2)}) collective-permute-start(bf16[160,384]{1,0:T(8,128)(2,1)S(1)} %convolution_convert_fusion.3), channel_id=1, source_target_pairs={{0,2},{2,4},{4,6},{6,8},{8,10},{10,12},{12,14},{14,0},{1,3},{3,5},... | collective-permute-start | bytes 368648 | tf_op jit(solution)/shard_map/ppermute | solution.py:20
  133.6 14.2 %collective-permute-start.14 = (bf16[160,384]{1,0:T(8,128)(2,1)S(1)}, bf16[160,384]{1,0:T(8,128)(2,1)S(1)}, u32[]{:S(2)}, u32[]{:S(2)}) collective-permute-start(bf16[160,384]{1,0:T(8,128)(2,1)S(1)} %fusion.31), channel_id=1, source_target_pairs={{0,2},{2,4},{4,6},{6,8},{8,10},{10,12},{12,14},{14,0},{1,3},{3,5},... | collective-permute-start | bytes 368648 | tf_op jit(solution)/shard_map/ppermute | solution.py:20
  135.7 14.2 %collective-permute-start.10 = (bf16[160,384]{1,0:T(8,128)(2,1)S(1)}, bf16[160,384]{1,0:T(8,128)(2,1)S(1)}, u32[]{:S(2)}, u32[]{:S(2)}) collective-permute-start(bf16[160,384]{1,0:T(8,128)(2,1)S(1)} %fusion.29), channel_id=1, source_target_pairs={{0,14},{2,0},{4,2},{6,4},{8,6},{10,8},{12,10},{14,12},{1,15},{3,1}... | collective-permute-start | bytes 368648 | tf_op jit(solution)/shard_map/ppermute | solution.py:20
  141.4 14.2 %collective-permute-start.7 = (bf16[160,384]{1,0:T(8,128)(2,1)S(1)}, bf16[160,384]{1,0:T(8,128)(2,1)S(1)}, u32[]{:S(2)}, u32[]{:S(2)}) collective-permute-start(bf16[160,384]{1,0:T(8,128)(2,1)S(1)} %fusion.25), channel_id=1, source_target_pairs={{0,14},{2,0},{4,2},{6,4},{8,6},{10,8},{12,10},{14,12},{1,15},{3,1}... | collective-permute-start | bytes 368648 | tf_op jit(solution)/shard_map/ppermute | solution.py:20
  143.6 14.2 %collective-permute-start.3 = (bf16[160,384]{1,0:T(8,128)(2,1)S(1)}, bf16[160,384]{1,0:T(8,128)(2,1)S(1)}, u32[]{:S(2)}, u32[]{:S(2)}) collective-permute-start(bf16[160,384]{1,0:T(8,128)(2,1)S(1)} %fusion.23), channel_id=1, source_target_pairs={{0,2},{2,4},{4,6},{6,8},{8,10},{10,12},{12,14},{14,0},{1,3},{3,5},... | collective-permute-start | bytes 368648 | tf_op jit(solution)/shard_map/ppermute | solution.py:20
  148.1 22.8 %collective-permute-start.15 = (bf16[160,384]{1,0:T(8,128)(2,1)S(1)}, bf16[160,384]{1,0:T(8,128)(2,1)S(1)}, u32[]{:S(2)}, u32[]{:S(2)}) collective-permute-start(bf16[160,384]{1,0:T(8,128)(2,1)S(1)} %fusion.30), channel_id=1, source_target_pairs={{0,2},{2,4},{4,6},{6,8},{8,10},{10,12},{12,14},{14,0},{1,3},{3,5},... | collective-permute-start | bytes 368648 | tf_op jit(solution)/shard_map/ppermute | solution.py:20
  150.2 12.1 %collective-permute-start.11 = (bf16[160,384]{1,0:T(8,128)(2,1)S(1)}, bf16[160,384]{1,0:T(8,128)(2,1)S(1)}, u32[]{:S(2)}, u32[]{:S(2)}) collective-permute-start(bf16[160,384]{1,0:T(8,128)(2,1)S(1)} %fusion.28), channel_id=1, source_target_pairs={{0,14},{2,0},{4,2},{6,4},{8,6},{10,8},{12,10},{14,12},{1,15},{3,1}... | collective-permute-start | bytes 368648 | tf_op jit(solution)/shard_map/ppermute | solution.py:20
  155.9 16.4 %collective-permute-start.8 = (bf16[160,384]{1,0:T(8,128)(2,1)S(1)}, bf16[160,384]{1,0:T(8,128)(2,1)S(1)}, u32[]{:S(2)}, u32[]{:S(2)}) collective-permute-start(bf16[160,384]{1,0:T(8,128)(2,1)S(1)} %fusion.24), channel_id=1, source_target_pairs={{0,14},{2,0},{4,2},{6,4},{8,6},{10,8},{12,10},{14,12},{1,15},{3,1}... | collective-permute-start | bytes 368648 | tf_op jit(solution)/shard_map/ppermute | solution.py:20
  158.0 10.7 %collective-permute-start.4 = (bf16[160,384]{1,0:T(8,128)(2,1)S(1)}, bf16[160,384]{1,0:T(8,128)(2,1)S(1)}, u32[]{:S(2)}, u32[]{:S(2)}) collective-permute-start(bf16[160,384]{1,0:T(8,128)(2,1)S(1)} %fusion.22), channel_id=1, source_target_pairs={{0,2},{2,4},{4,6},{6,8},{8,10},{10,12},{12,14},{14,0},{1,3},{3,5},... | collective-permute-start | bytes 368648 | tf_op jit(solution)/shard_map/ppermute | solution.py:20
  162.5 9.6 %collective-permute-start.12 = (bf16[160,384]{1,0:T(8,128)(2,1)S(1)}, bf16[160,384]{1,0:T(8,128)(2,1)S(1)}, u32[]{:S(2)}, u32[]{:S(2)}) collective-permute-start(bf16[160,384]{1,0:T(8,128)(2,1)S(1)} %fusion.27), channel_id=1, source_target_pairs={{0,14},{2,0},{4,2},{6,4},{8,6},{10,8},{12,10},{14,12},{1,15},{3,1}... | collective-permute-start | bytes 368648 | tf_op jit(solution)/shard_map/ppermute | solution.py:20
  168.9 9.2 %collective-permute-start.5 = (bf16[160,384]{1,0:T(8,128)(2,1)S(1)}, bf16[160,384]{1,0:T(8,128)(2,1)S(1)}, u32[]{:S(2)}, u32[]{:S(2)}) collective-permute-start(bf16[160,384]{1,0:T(8,128)(2,1)S(1)} %fusion.21), channel_id=1, source_target_pairs={{0,2},{2,4},{4,6},{6,8},{8,10},{10,12},{12,14},{14,0},{1,3},{3,5},... | collective-permute-start | bytes 368648 | tf_op jit(solution)/shard_map/ppermute | solution.py:20
  178.3 18.8 %copy-start.1 = (f32[128,2]{0,1:T(2,128)S(1)}, f32[128,2]{0,1:T(2,128)}, u32[]{:S(2)}) copy-start(f32[128,2]{0,1:T(2,128)} %param.7) | copy-start | bytes 3076
  179.9 29.2 %all-to-all-start.1 = ((bf16[64,16,128]{2,1,0:T(8,128)(2,1)}), bf16[64,16,128]{2,1,0:T(8,128)(2,1)S(1)}, u32[]{:S(2)}, u32[]{:S(2)}) async-start(bf16[64,16,128]{2,1,0:T(8,128)(2,1)} %bitcast.29), calls=%async_computation.1 | async-start | bytes 524288 | tf_op jit(solution)/shard_map/all_to_all | solution.py:126
